TPU v7x, 32 devices: a whole 2x2x4 slice. The times are simulated.
32 devices in a mesh: dp: 8 (over z, x), mp: 4 (over y, core).
Axes of the slice: x: 2, y: 2, z: 4, core: 2. Of those that a mesh axis runs over, the one named last changes fastest.
Arguments:
- tokens: bfloat16 [8192, 2048], P('dp', 'mp'), may hold values from -6 to 6
- norm_gain: bfloat16 [2048], replicated, may hold values from 0.099609375 to 1.8984375
- wi_gate: bfloat16 [2048, 5120], P(None, 'mp'), may hold values from -0.125 to 0.125
- wi_linear: bfloat16 [2048, 5120], P(None, 'mp'), may hold values from -0.125 to 0.125
- wo_out: bfloat16 [5120, 2048], P('mp'), may hold values from -0.078125 to 0.078125
- task_table: float32 [8, 64], replicated, may hold values from -5 to 5
- layer_table: float32 [24, 64], replicated, may hold values from -5 to 5
- task_ids: int32 [64], P('dp'), may hold values from 0 to 7
- layer_index: int32 [1], replicated, may hold values from 0 to 23
- hyper_in: bfloat16 [128, 1024], P(None, 'mp'), may hold values from -0.5 to 0.5
- gen_down: bfloat16 [1024, 131072], P(None, ('mp', 'dp')), may hold values from -0.0078125 to 0.0078125
- gen_up: bfloat16 [1024, 131072], P(None, ('mp', 'dp')), may hold values from -0.046875 to 0.046875
Outputs:
- mixed: bfloat16 [8192, 2048], P('dp', 'mp')
All inputs are finite; a program needn't handle non-finite values.
Results may differ from a plain program's by a relative error of at most 0.019.
Values may be sent and summed in bfloat16 or wider, within the bound.
A program may use at most 128 MiB of HBM per device.

v0:
```python
import jax
import jax.numpy as jnp
from jax import lax
from jax.sharding import PartitionSpec as P

R = 64


def matmul(left, right):
    return jnp.dot(left, right, preferred_element_type=jnp.float32)


def per_device(
    tokens,
    norm_gain,
    wi_gate,
    wi_linear,
    wo_out,
    task_table,
    layer_table,
    task_ids,
    layer_index,
    hyper_in,
    gen_down,
    gen_up,
):
    task_count = task_table.shape[0]
    layer_row = jnp.take(layer_table, layer_index, axis=0)
    embed = jnp.concatenate(
        [task_table, jnp.broadcast_to(layer_row, (task_count, layer_row.shape[1]))], axis=1
    ).astype(jnp.bfloat16)
    hidden_part = jnp.maximum(matmul(embed, hyper_in), 0.0).astype(jnp.bfloat16)
    hidden = lax.all_gather(hidden_part, "mp", axis=1, tiled=True)
    every_id = lax.all_gather(task_ids, "dp", axis=0, tiled=True)
    wanted = jnp.take(hidden, every_id, axis=0)
    made = (
        matmul(wanted, gen_down).astype(jnp.bfloat16),
        matmul(wanted, gen_up).astype(jnp.bfloat16),
    )
    local_down, local_up = (
        lax.all_to_all(made[0], "dp", split_axis=0, concat_axis=1, tiled=True),
        lax.all_to_all(made[1], "dp", split_axis=0, concat_axis=1, tiled=True),
    )
    full_rows = lax.all_gather(tokens, "mp", axis=1, tiled=True)
    wide = full_rows.astype(jnp.float32)
    scale = lax.rsqrt(jnp.mean(wide * wide, axis=-1, keepdims=True) + 1e-06)
    normed = (wide * scale * norm_gain.astype(jnp.float32)).astype(jnp.bfloat16)
    gate = matmul(normed, wi_gate)
    linear = matmul(normed, wi_linear)
    act = (jax.nn.gelu(gate, approximate=True) * linear).astype(jnp.bfloat16)
    seqs_dev = task_ids.shape[0]
    tok_dev = tokens.shape[0]
    seq_len = tok_dev // seqs_dev
    partial_sums = matmul(act, wo_out)
    ffout = lax.psum_scatter(
        partial_sums.astype(jnp.bfloat16), "mp", scatter_dimension=1, tiled=True
    )
    down_block = local_down.reshape(seqs_dev, -1, R)
    up_block = local_up.reshape(seqs_dev, -1, R)
    blocks = ffout.reshape(seqs_dev, seq_len, -1)
    squeeze_part = jnp.einsum(
        "std,sdr->str", blocks, down_block, preferred_element_type=jnp.float32
    )
    squeeze_full = lax.psum(squeeze_part.astype(jnp.bfloat16), "mp").astype(jnp.float32)
    squeezed = jnp.maximum(squeeze_full, 0.0).astype(jnp.bfloat16)
    expand = jnp.einsum("str,sdr->std", squeezed, up_block, preferred_element_type=jnp.float32)
    total = tokens.astype(jnp.float32) + ffout.astype(jnp.float32) + expand.reshape(tok_dev, -1)
    return total.astype(jnp.bfloat16)


def solution(mesh):
    return jax.shard_map(
        per_device,
        mesh=mesh,
        in_specs=(
            P("dp", "mp"),
            P(),
            P(None, "mp"),
            P(None, "mp"),
            P("mp", None),
            P(),
            P(),
            P("dp"),
            P(),
            P(None, "mp"),
            P(None, ("mp", "dp")),
            P(None, ("mp", "dp")),
        ),
        out_specs=P("dp", "mp"),
        check_vma=False,
    )
```

profile of v0, /device:TPU:0, one launch (start us, length us, event | category | flops | bytes accessed | tf_op | source)
XLA Modules:
  0.0 174.6 jit_solution(7065484068272233757)
XLA Ops:
  6.5 0.0 copy-start
  6.5 0.0 all-gather.2.cloned.1.call-start
  6.5 0.7 all-gather.2.cloned.1.call-update
  7.3 0.0 reduce-scatter.2.cloned.1.call-start
  7.3 0.7 convert_element_type.45
  8.0 38.1 %all-gather.2.cloned.1.call-done = bf16[1024,2048]{1,0:T(8,128)(2,1)} async-done(((bf16[1024,512]{1,0:T(8,128)(2,1)}), bf16[1024,2048]{1,0:T(8,128)(2,1)}) %all-gather.2.cloned.1.call-update) | async-done | bytes 4194320 | tf_op jit(solution)/shard_map/all_gather | solution.py:44
  46.1 3.1 %fusion = f32[1024]{0:T(1024)S(1)} fusion(bf16[1024,2048]{1,0:T(8,128)(2,1)} %all-gather.2.cloned.1.call-done), kind=kLoop, calls=%fused_computation.3 | loop fusion | flops 6290432 | bytes 4198400 | tf_op jit(solution)/shard_map/reduce_sum | solution.py:46
  49.2 10.7 %fusion.16 = f32[1024,1280]{1,0:T(8,128)} fusion(bf16[2048,1280]{1,0:T(8,128)(2,1)} %param.14, bf16[1024,2048]{1,0:T(8,128)(2,1)} %all-gather.2.cloned.1.call-done, f32[2048]{0:T(1024)S(1)} %convert_element_type.45, f32[1024]{0:T(1024)S(1)} %add_rsqrt_fusion), kind=kOutput, calls=%fused_computation.23 | convolution fusion | flops 5377097728 | bytes 14692352 | tf_op jit(solution)/shard_map/dot_general | solution.py:10
  59.9 0.0 copy-start.3
  59.9 0.0 copy-start.5
  59.9 0.0 copy-start.4
  59.9 19.9 %convolution_convert_fusion.2 = bf16[1024,2048]{1,0:T(8,128)(2,1)} fusion(bf16[1280,2048]{1,0:T(8,128)(2,1)} %param.16, f32[1024,1280]{1,0:T(8,128)} %fusion.16, bf16[2048,1280]{1,0:T(8,128)(2,1)} %param.15, bf16[1024,2048]{1,0:T(8,128)(2,1)} %all-gather.2.cloned.1.call-done, f32[2048]{0:T(1024)S(1)} %convert_element_type.45, f32[1024]{0:T(1024)S(1)} %add_rsqrt_fusion), kind=kOutput, calls=%fused_computation.20 | convolution fusion | flops 10761011200 | bytes 24129536 | tf_op jit(solution)/shard_map/dot_general | solution.py:10
  79.8 0.0 reduce-scatter.2.cloned.1.call-update
  80.5 0.0 copy-done.3
  80.5 0.7 fusion.27
  81.2 0.1 pad.3.clone
  81.3 0.0 copy-done.5
  81.3 0.6 dynamic-slice.4
  82.6 0.0 copy-done.4
  82.6 0.2 dynamic-update-slice.1
  82.8 11.4 %all-reduce = s32[64]{0:T(128)S(1)} all-reduce(s32[64]{0:T(128)S(1)} %dynamic-update-slice.1), channel_id=1, replica_groups=mesh['dp'=8,'mp'=4] {'dp'}, use_global_device_ids=true, to_apply=%add | all-reduce | flops 64 | bytes 512
  94.2 0.0 copy-done
  94.2 0.1 fusion.18
  94.3 5.2 %all_gather.11 = bf16[8,1024]{1,0:T(8,128)(2,1)S(1)} all-gather(bf16[8,256]{1,0:T(8,128)(2,1)S(1)} %fusion.18), channel_id=1, replica_groups=mesh['dp'=8,'mp'=4] {'mp'}, dimensions={1}, use_global_device_ids=true | all-gather | bytes 20480 | tf_op jit(solution)/shard_map/all_gather | solution.py:33
  99.5 0.7 gather_fusion
  100.2 5.8 %fusion.12 = bf16[8,8,4096]{2,1,0:T(8,128)(2,1)} fusion(bf16[1024,4096]{1,0:T(8,128)(2,1)} %param.22, bf16[64,1024]{1,0:T(8,128)(2,1)S(1)} %gather_fusion, pred[64]{0:T(512)(128)(4,1)S(1)} %compare_and_fusion), kind=kOutput, calls=%fused_computation.18 | convolution fusion | flops 537198592 | bytes 9044032 | tf_op jit(solution)/shard_map/dot_general | solution.py:10
  106.1 3.5 %all-to-all-start = ((bf16[8,8,4096]{2,1,0:T(8,128)(2,1)}), bf16[8,8,4096]{2,1,0:T(8,128)(2,1)S(1)}, u32[]{:S(2)}, u32[]{:S(2)}) async-start(bf16[8,8,4096]{2,1,0:T(8,128)(2,1)} %fusion.12), calls=%async_computation.1 | async-start | bytes 1048576 | tf_op jit(solution)/shard_map/all_to_all | solution.py:41
  109.6 5.8 %fusion.13 = bf16[8,8,4096]{2,1,0:T(8,128)(2,1)} fusion(bf16[1024,4096]{1,0:T(8,128)(2,1)} %param.23, bf16[64,1024]{1,0:T(8,128)(2,1)S(1)} %gather_fusion, pred[64]{0:T(512)(128)(4,1)S(1)} %compare_and_fusion), kind=kOutput, calls=%fused_computation.19 | convolution fusion | flops 537198592 | bytes 9044032 | tf_op jit(solution)/shard_map/dot_general | solution.py:10
  115.4 9.4 %all-to-all-done = bf16[8,8,4096]{2,1,0:T(8,128)(2,1)S(1)} async-done(((bf16[8,8,4096]{2,1,0:T(8,128)(2,1)}), bf16[8,8,4096]{2,1,0:T(8,128)(2,1)S(1)}, u32[]{:S(2)}, u32[]{:S(2)}) %all-to-all-start) | async-done | bytes 524320 | tf_op jit(solution)/shard_map/all_to_all | solution.py:41
  124.8 4.3 %all-to-all-start.1 = ((bf16[8,8,4096]{2,1,0:T(8,128)(2,1)}), bf16[8,8,4096]{2,1,0:T(8,128)(2,1)}, u32[]{:S(2)}, u32[]{:S(2)}) async-start(bf16[8,8,4096]{2,1,0:T(8,128)(2,1)} %fusion.13), calls=%async_computation.2 | async-start | bytes 1048576 | tf_op jit(solution)/shard_map/all_to_all | solution.py:42
  129.1 0.0 all-reduce.3.cloned.1.call-start
  129.1 0.0 copy-start.1
  129.1 0.3 copy.16
  129.4 1.1 reshape.46
  130.6 0.0 reduce-scatter.2.cloned.1.call-done
  130.6 0.0 copy-start.2
  130.6 2.5 %convolution_convert_fusion.3 = bf16[8,128,64]{1,2,0:T(8,128)(2,1)} fusion(bf16[8,128,512]{2,1,0:T(8,128)(2,1)} %bitcast.25, bf16[8,512,64]{2,1,0:T(8,128)(2,1)S(1)} %reshape.46), kind=kOutput, calls=%fused_computation.24 | convolution fusion | flops 67174400 | bytes 1703936 | tf_op jit(solution)/shard_map/std,sdr->str/dot_general | solution.py:61
  133.1 0.0 all-reduce.3.cloned.1.call-update
  133.1 10.2 %all-to-all-done.1 = bf16[8,8,4096]{2,1,0:T(8,128)(2,1)} async-done(((bf16[8,8,4096]{2,1,0:T(8,128)(2,1)}), bf16[8,8,4096]{2,1,0:T(8,128)(2,1)}, u32[]{:S(2)}, u32[]{:S(2)}) %all-to-all-start.1) | async-done | bytes 524320 | tf_op jit(solution)/shard_map/all_to_all | solution.py:42
  143.3 2.1 %copy.18 = bf16[8,8,4096]{2,1,0:T(8,128)(2,1)} copy(bf16[8,8,4096]{2,0,1:T(8,128)(2,1)} %bitcast.8) | data formatting | bytes 1048576 | tf_op jit(solution)/shard_map/all_to_all | solution.py:42
  145.4 2.1 %reshape.47 = bf16[8,512,64]{2,1,0:T(8,128)(2,1)S(1)} reshape(bf16[8,8,4096]{2,1,0:T(8,128)(2,1)} %copy.18) | data formatting | bytes 1048576 | tf_op jit(solution)/shard_map/reshape | solution.py:59
  147.5 17.7 %all-reduce.3.cloned.1.call-done = bf16[8,128,64]{1,2,0:T(8,128)(2,1)} async-done(((bf16[8,128,64]{1,2,0:T(8,128)(2,1)}), bf16[8,128,64]{1,2,0:T(8,128)(2,1)}) %all-reduce.3.cloned.1.call-update) | async-done | bytes 131088 | tf_op jit(solution)/shard_map/psum | solution.py:64
  165.2 1.4 fusion.21
  166.6 0.0 copy-done.1
  166.6 0.0 copy-done.2
  166.6 1.4 fusion.14
  (6 shorter events, 0.0 us)
Async XLA Ops:
  6.5 87.6 %copy-start = (bf16[128,256]{1,0:T(8,128)(2,1)S(1)}, bf16[128,256]{1,0:T(8,128)(2,1)}, u32[]{:S(2)}) copy-start(bf16[128,256]{1,0:T(8,128)(2,1)} %param.21) | copy-start | bytes 196612
  6.5 39.6 %all-gather.2.cloned.1.call-start = ((), (), s32[]{:S(2)}) async-start(), calls=%async_computation.3 | async-start | bytes 5242880 | tf_op jit(solution)/shard_map/all_gather | solution.py:44
  7.3 123.3 %reduce-scatter.2.cloned.1.call-start = ((), (), s32[]{:S(2)}) async-start(), calls=%async_computation.4 | async-start | bytes 5242880 | tf_op jit(solution)/shard_map/reduce_scatter | solution.py:55
  59.9 20.6 %copy-start.3 = (f32[8,64]{1,0:T(8,128)S(1)}, f32[8,64]{1,0:T(8,128)}, u32[]{:S(2)}) copy-start(f32[8,64]{1,0:T(8,128)} %param.17) | copy-start | bytes 6148
  59.9 21.4 %copy-start.5 = (u32[32]{0:T(128)S(1)}, u32[32]{0:T(128)}, u32[]{:S(2)}) copy-start(u32[32]{0:T(128)} %constant.73) | copy-start | bytes 388
  59.9 22.7 %copy-start.4 = (s32[8]{0:T(128)S(1)}, s32[8]{0:T(128)}, u32[]{:S(2)}) copy-start(s32[8]{0:T(128)} %param.19) | copy-start | bytes 100
  106.1 18.7 %all-to-all-start = ((bf16[8,8,4096]{2,1,0:T(8,128)(2,1)}), bf16[8,8,4096]{2,1,0:T(8,128)(2,1)S(1)}, u32[]{:S(2)}, u32[]{:S(2)}) async-start(bf16[8,8,4096]{2,1,0:T(8,128)(2,1)} %fusion.12), calls=%async_computation.1 | async-start | bytes 1048576 | tf_op jit(solution)/shard_map/all_to_all | solution.py:41
  124.8 18.6 %all-to-all-start.1 = ((bf16[8,8,4096]{2,1,0:T(8,128)(2,1)}), bf16[8,8,4096]{2,1,0:T(8,128)(2,1)}, u32[]{:S(2)}, u32[]{:S(2)}) async-start(bf16[8,8,4096]{2,1,0:T(8,128)(2,1)} %fusion.13), calls=%async_computation.2 | async-start | bytes 1048576 | tf_op jit(solution)/shard_map/all_to_all | solution.py:42
  129.1 36.1 %all-reduce.3.cloned.1.call-start = ((), (), s32[]{:S(2)}) async-start(), calls=%async_computation.5 | async-start | bytes 262144 | tf_op jit(solution)/shard_map/psum | solution.py:64
  129.1 37.5 %copy-start.1 = (bf16[1024,512]{1,0:T(8,128)(2,1)S(1)}, bf16[1024,512]{1,0:T(8,128)(2,1)}, u32[]{:S(2)}) copy-start(bf16[1024,512]{1,0:T(8,128)(2,1)} %param.12) | copy-start | bytes 3145732
  130.6 36.0 %copy-start.2 = (bf16[1024,512]{1,0:T(8,128)(2,1)S(1)}, bf16[1024,512]{1,0:T(8,128)(2,1)}, u32[]{:S(2)}) copy-start(bf16[1024,512]{1,0:T(8,128)(2,1)} %reduce-scatter.2.cloned.1.call-done) | copy-start | bytes 3145732
Sparse Core Ops, SparseCore 0:
  8.9 37.1 all-gather.1
  80.0 44.3 reduce-scatter.1
  133.2 31.9 all-reduce.2
where the time goes:
time: 175 us
  waiting for transfers between devices  76.2 us (44%)
  matrix products  46.2 us (26%)
  blocking collectives  16.6 us (9%)
  between operations  14.6 us (8%)
  starting transfers between devices  7.9 us (5%)
  local copies, waits for them, and re-layouts  7.23 us (4%)
  other arithmetic  5.92 us (3%)
    dot_general x5, matrix products, matmul(): return jnp.dot(left, right, preferred_element_type=jnp.float32)  42.4 us
    all_gather x1, waiting for transfers between devices, per_device(): full_rows = lax.all_gather(tokens, 'mp', axis=1, tiled=True)  38.1 us
    psum x1, waiting for transfers between devices, per_device(): lax.psum(squeeze_part.astype(jnp.bfloat16), 'mp').astype(jnp.float32)  17.7 us
    unnamed x1, blocking collectives  11.4 us
    all_to_all x1, waiting for transfers between devices, per_device(): lax.all_to_all(made[1], 'dp', split_axis=0, concat_axis=1, tiled=True)  10.2 us
    all_to_all x1, waiting for transfers between devices, per_device(): lax.all_to_all(made[0], 'dp', split_axis=0, concat_axis=1, tiled=True)  9.39 us
    all_gather x1, blocking collectives, per_device(): hidden = lax.all_gather(hidden_part, 'mp', axis=1, tiled=True)  5.2 us
    all_to_all x1, starting transfers between devices, per_device(): lax.all_to_all(made[1], 'dp', split_axis=0, concat_axis=1, tiled=True)  4.33 us
  transfers between devices with their start and end apart: 5, of which 4 were waited for; matrix products, arithmetic and copies ran while one was open for 13% of the time, Pallas kernels for 0%

commit v1 on v0

--- a/solution.py
+++ b/solution.py
@@ -41,7 +41,7 @@
         lax.all_to_all(made[0], "dp", split_axis=0, concat_axis=1, tiled=True),
         lax.all_to_all(made[1], "dp", split_axis=0, concat_axis=1, tiled=True),
     )
-    full_rows = lax.all_gather(tokens, "mp", axis=1, tiled=True)
+    full_rows = jnp.concatenate(lax.all_gather(tokens, "mp"), axis=1)
     wide = full_rows.astype(jnp.float32)
     scale = lax.rsqrt(jnp.mean(wide * wide, axis=-1, keepdims=True) + 1e-06)
     normed = (wide * scale * norm_gain.astype(jnp.float32)).astype(jnp.bfloat16)

time: 175 us -> 195 us (1.11)
  local copies, waits for them, and re-layouts: 7.23 us -> 18.2 us
  other arithmetic: 5.92 us -> 14.4 us
    convert_element_type x0 -> x1, local copies, waits for them, and re-layouts: none -> 8.74 us  [per_device(): wide = full_rows.astype(jnp.float32)]
    convert_element_type x0 -> x1, other arithmetic: none -> 4.41 us  [per_device(): wide = full_rows.astype(jnp.float32)]
    convert_element_type x1 -> x2, other arithmetic: 0.69 us -> 4.59 us  [per_device(): normed = (wide * scale * norm_gain.astype(jnp.float32)).astype(jnp.bfloat16)]
    unnamed x15 -> x19, local copies, waits for them, and re-layouts: 0.85 us -> 3.12 us
  transfers between devices with their start and end apart: 5 -> 5, of which waited for: 4 -> 4; matrix products, arithmetic and copies ran while one was open for 13% -> 12% of each run, Pallas kernels for 0% -> 0%
where the time goes in v1:
time: 195 us; the launch traced here: 194 us
  waiting for transfers between devices  76.4 us (39%)
  matrix products  46.2 us (24%)
  local copies, waits for them, and re-layouts  18.2 us (9%)
  blocking collectives  16.7 us (9%)
  between operations  14.6 us (7%)
  other arithmetic  14.4 us (7%)
  starting transfers between devices  7.72 us (4%)
    dot_general x5, matrix products, matmul(): return jnp.dot(left, right, preferred_element_type=jnp.float32)  42.4 us
    all_gather x1, waiting for transfers between devices, per_device(): full_rows = jnp.concatenate(lax.all_gather(tokens, 'mp'), axis=1)  38.1 us
    psum x1, waiting for transfers between devices, per_device(): lax.psum(squeeze_part.astype(jnp.bfloat16), 'mp').astype(jnp.float32)  17.7 us
    unnamed x1, blocking collectives  11.4 us
    all_to_all x1, waiting for transfers between devices, per_device(): lax.all_to_all(made[1], 'dp', split_axis=0, concat_axis=1, tiled=True)  10.4 us
    all_to_all x1, waiting for transfers between devices, per_device(): lax.all_to_all(made[0], 'dp', split_axis=0, concat_axis=1, tiled=True)  9.39 us
    convert_element_type x1, local copies, waits for them, and re-layouts, per_device(): wide = full_rows.astype(jnp.float32)  8.74 us
    all_gather x1, blocking collectives, per_device(): hidden = lax.all_gather(hidden_part, 'mp', axis=1, tiled=True)  5.38 us
  transfers between devices with their start and end apart: 5, of which 4 were waited for; matrix products, arithmetic and copies ran while one was open for 12% of the time, Pallas kernels for 0%

profile of v1, /device:TPU:0, one launch (start us, length us, event | category | flops | bytes accessed | tf_op | source)
XLA Modules:
  0.0 194.2 jit_solution(4731422604779952723)
XLA Ops:
  6.5 0.0 copy-start
  6.5 0.0 all-gather.3.cloned.1.call-start
  6.5 0.7 all-gather.3.cloned.1.call-update
  7.3 0.0 reduce-scatter.2.cloned.1.call-start
  7.3 0.7 convert_element_type.58
  8.0 38.1 %all-gather.3.cloned.1.call-done = bf16[4096,512]{1,0:T(8,128)(2,1)} async-done(((bf16[1024,512]{1,0:T(8,128)(2,1)}), bf16[4096,512]{1,0:T(8,128)(2,1)}) %all-gather.3.cloned.1.call-update) | async-done | bytes 4194320 | tf_op jit(solution)/shard_map/all_gather | solution.py:44
  46.1 0.0 copy-start.1
  46.1 3.2 %fusion = f32[1024]{0:T(1024)S(1)} fusion(bf16[4,1024,512]{2,1,0:T(8,128)(2,1)} %bitcast.47), kind=kLoop, calls=%fused_computation.3 | loop fusion | flops 6290432 | bytes 4198400 | tf_op jit(solution)/shard_map/reduce_sum | solution.py:46
  49.3 0.2 copy-done.1
  49.6 4.4 %convert_bitcast_fusion = f32[1024,4,512]{2,0,1:T(8,128)} fusion(bf16[4096,512]{1,0:T(8,128)(2,1)S(1)} %copy-done.1), kind=kLoop, calls=%fused_computation.2 | loop fusion | flops 2097152 | bytes 12582912 | tf_op jit(solution)/shard_map/convert_element_type | solution.py:45
  54.0 8.7 %copy.21 = f32[1024,4,512]{0,2,1:T(8,128)} copy(f32[1024,4,512]{2,0,1:T(8,128)} %convert_bitcast_fusion) | data formatting | bytes 16777216 | tf_op jit(solution)/shard_map/convert_element_type | solution.py:45
  62.7 3.9 %fusion.2 = bf16[1024,2048]{0,1:T(8,128)(2,1)S(1)} fusion(f32[1024,4,512]{0,2,1:T(8,128)} %copy.21, f32[2048]{0:T(1024)S(1)} %convert_element_type.58, f32[1024]{0:T(1024)S(1)} %add_rsqrt_fusion), kind=kLoop, calls=%fused_computation.6 | loop fusion | flops 6291456 | bytes 12595200 | tf_op jit(solution)/shard_map/convert_element_type | solution.py:47
  66.6 0.0 copy-start.2
  66.6 2.1 %copy-done.2 = bf16[1024,2048]{0,1:T(8,128)(2,1)} copy-done((bf16[1024,2048]{0,1:T(8,128)(2,1)}, bf16[1024,2048]{0,1:T(8,128)(2,1)S(1)}, u32[]{:S(2)}) %copy-start.2) | copy-done | bytes 4194328
  68.7 10.0 %fusion.27 = f32[1024,1280]{1,0:T(8,128)} fusion(bf16[1024,2048]{0,1:T(8,128)(2,1)S(1)} %fusion.2, bf16[2048,1280]{1,0:T(8,128)(2,1)} %param.14), kind=kOutput, calls=%fused_computation.45 | convolution fusion | flops 5368709120 | bytes 14680064 | tf_op jit(solution)/shard_map/dot_general | solution.py:10
  78.7 0.0 copy-start.5
  78.7 0.0 copy-start.7
  78.7 0.0 copy-start.6
  78.7 20.6 %convolution_convert_fusion.2 = bf16[1024,2048]{1,0:T(8,128)(2,1)} fusion(bf16[1280,2048]{1,0:T(8,128)(2,1)} %param.16, f32[1024,1280]{1,0:T(8,128)} %fusion.27, bf16[1024,2048]{0,1:T(8,128)(2,1)} %copy-done.2, bf16[2048,1280]{1,0:T(8,128)(2,1)} %param.15), kind=kOutput, calls=%fused_computation.21 | convolution fusion | flops 10752622592 | bytes 24117248 | tf_op jit(solution)/shard_map/dot_general | solution.py:10
  99.3 0.0 reduce-scatter.2.cloned.1.call-update
  100.0 0.0 copy-done.5
  100.0 0.0 copy-done.7
  100.0 0.6 dynamic-slice.4
  101.3 0.7 fusion.22
  102.0 0.1 pad.3.clone
  102.1 0.0 copy-done.6
  102.1 0.2 dynamic-update-slice.1
  102.3 11.4 %all-reduce = s32[64]{0:T(128)S(1)} all-reduce(s32[64]{0:T(128)S(1)} %dynamic-update-slice.1), channel_id=1, replica_groups=mesh['dp'=8,'mp'=4] {'dp'}, use_global_device_ids=true, to_apply=%add | all-reduce | flops 64 | bytes 512
  113.6 0.0 copy-done
  113.6 0.1 fusion.15
  113.8 5.4 %all_gather.15 = bf16[8,1024]{1,0:T(8,128)(2,1)S(1)} all-gather(bf16[8,256]{1,0:T(8,128)(2,1)S(1)} %fusion.15), channel_id=1, replica_groups=mesh['dp'=8,'mp'=4] {'mp'}, dimensions={1}, use_global_device_ids=true | all-gather | bytes 20480 | tf_op jit(solution)/shard_map/all_gather | solution.py:33
  119.1 0.7 gather_fusion
  119.9 5.8 %fusion.12 = bf16[8,8,4096]{2,1,0:T(8,128)(2,1)} fusion(bf16[1024,4096]{1,0:T(8,128)(2,1)} %param.22, bf16[64,1024]{1,0:T(8,128)(2,1)S(1)} %gather_fusion, pred[64]{0:T(512)(128)(4,1)S(1)} %compare_and_fusion), kind=kOutput, calls=%fused_computation.19 | convolution fusion | flops 537198592 | bytes 9044032 | tf_op jit(solution)/shard_map/dot_general | solution.py:10
  125.7 3.5 %all-to-all-start = ((bf16[8,8,4096]{2,1,0:T(8,128)(2,1)}), bf16[8,8,4096]{2,1,0:T(8,128)(2,1)S(1)}, u32[]{:S(2)}, u32[]{:S(2)}) async-start(bf16[8,8,4096]{2,1,0:T(8,128)(2,1)} %fusion.12), calls=%async_computation.1 | async-start | bytes 1048576 | tf_op jit(solution)/shard_map/all_to_all | solution.py:41
  129.2 5.8 %fusion.13 = bf16[8,8,4096]{2,1,0:T(8,128)(2,1)} fusion(bf16[1024,4096]{1,0:T(8,128)(2,1)} %param.23, bf16[64,1024]{1,0:T(8,128)(2,1)S(1)} %gather_fusion, pred[64]{0:T(512)(128)(4,1)S(1)} %compare_and_fusion), kind=kOutput, calls=%fused_computation.20 | convolution fusion | flops 537198592 | bytes 9044032 | tf_op jit(solution)/shard_map/dot_general | solution.py:10
  135.0 9.4 %all-to-all-done = bf16[8,8,4096]{2,1,0:T(8,128)(2,1)S(1)} async-done(((bf16[8,8,4096]{2,1,0:T(8,128)(2,1)}), bf16[8,8,4096]{2,1,0:T(8,128)(2,1)S(1)}, u32[]{:S(2)}, u32[]{:S(2)}) %all-to-all-start) | async-done | bytes 524320 | tf_op jit(solution)/shard_map/all_to_all | solution.py:41
  144.4 4.1 %all-to-all-start.1 = ((bf16[8,8,4096]{2,1,0:T(8,128)(2,1)}), bf16[8,8,4096]{2,1,0:T(8,128)(2,1)}, u32[]{:S(2)}, u32[]{:S(2)}) async-start(bf16[8,8,4096]{2,1,0:T(8,128)(2,1)} %fusion.13), calls=%async_computation.2 | async-start | bytes 1048576 | tf_op jit(solution)/shard_map/all_to_all | solution.py:42
  148.5 0.0 all-reduce.3.cloned.1.call-start
  148.6 0.0 copy-start.3
  148.6 0.3 copy.22
  148.9 1.1 reshape.50
  150.0 0.0 reduce-scatter.2.cloned.1.call-done
  150.1 0.0 copy-start.4
  150.1 2.5 %convolution_convert_fusion.3 = bf16[8,128,64]{1,2,0:T(8,128)(2,1)} fusion(bf16[8,128,512]{2,1,0:T(8,128)(2,1)} %bitcast.48, bf16[8,512,64]{2,1,0:T(8,128)(2,1)S(1)} %reshape.50), kind=kOutput, calls=%fused_computation.24 | convolution fusion | flops 67174400 | bytes 1703936 | tf_op jit(solution)/shard_map/std,sdr->str/dot_general | solution.py:61
  152.6 0.0 all-reduce.3.cloned.1.call-update
  152.6 10.4 %all-to-all-done.1 = bf16[8,8,4096]{2,1,0:T(8,128)(2,1)} async-done(((bf16[8,8,4096]{2,1,0:T(8,128)(2,1)}), bf16[8,8,4096]{2,1,0:T(8,128)(2,1)}, u32[]{:S(2)}, u32[]{:S(2)}) %all-to-all-start.1) | async-done | bytes 524320 | tf_op jit(solution)/shard_map/all_to_all | solution.py:42
  163.0 2.1 %copy.24 = bf16[8,8,4096]{2,1,0:T(8,128)(2,1)} copy(bf16[8,8,4096]{2,0,1:T(8,128)(2,1)} %bitcast.12) | data formatting | bytes 1048576 | tf_op jit(solution)/shard_map/all_to_all | solution.py:42
  165.1 2.1 %reshape.51 = bf16[8,512,64]{2,1,0:T(8,128)(2,1)S(1)} reshape(bf16[8,8,4096]{2,1,0:T(8,128)(2,1)} %copy.24) | data formatting | bytes 1048576 | tf_op jit(solution)/shard_map/reshape | solution.py:59
  167.1 17.7 %all-reduce.3.cloned.1.call-done = bf16[8,128,64]{1,2,0:T(8,128)(2,1)} async-done(((bf16[8,128,64]{1,2,0:T(8,128)(2,1)}), bf16[8,128,64]{1,2,0:T(8,128)(2,1)}) %all-reduce.3.cloned.1.call-update) | async-done | bytes 131088 | tf_op jit(solution)/shard_map/psum | solution.py:64
  184.9 1.4 fusion.16
  186.2 0.0 copy-done.3
  186.3 0.0 copy-done.4
  186.3 1.4 fusion.14
  (6 shorter events, 0.0 us)
Async XLA Ops:
  6.5 107.1 %copy-start = (bf16[128,256]{1,0:T(8,128)(2,1)S(1)}, bf16[128,256]{1,0:T(8,128)(2,1)}, u32[]{:S(2)}) copy-start(bf16[128,256]{1,0:T(8,128)(2,1)} %param.21) | copy-start | bytes 196612
  6.5 39.6 %all-gather.3.cloned.1.call-start = ((), (), s32[]{:S(2)}) async-start(), calls=%async_computation.5 | async-start | bytes 5242880 | tf_op jit(solution)/shard_map/all_gather | solution.py:44
  7.3 142.8 %reduce-scatter.2.cloned.1.call-start = ((), (), s32[]{:S(2)}) async-start(), calls=%async_computation.3 | async-start | bytes 5242880 | tf_op jit(solution)/shard_map/reduce_scatter | solution.py:55
  46.1 3.4 %copy-start.1 = (bf16[4096,512]{1,0:T(8,128)(2,1)S(1)}, bf16[4096,512]{1,0:T(8,128)(2,1)}, u32[]{:S(2)}) copy-start(bf16[4096,512]{1,0:T(8,128)(2,1)} %all-gather.3.cloned.1.call-done) | copy-start | bytes 12582916
  66.6 2.1 %copy-start.2 = (bf16[1024,2048]{0,1:T(8,128)(2,1)}, bf16[1024,2048]{0,1:T(8,128)(2,1)S(1)}, u32[]{:S(2)}) copy-start(bf16[1024,2048]{0,1:T(8,128)(2,1)S(1)} %fusion.2) | copy-start | bytes 12582916
  78.7 21.3 %copy-start.5 = (f32[8,64]{1,0:T(8,128)S(1)}, f32[8,64]{1,0:T(8,128)}, u32[]{:S(2)}) copy-start(f32[8,64]{1,0:T(8,128)} %param.17) | copy-start | bytes 6148
  78.7 21.4 %copy-start.7 = (u32[32]{0:T(128)S(1)}, u32[32]{0:T(128)}, u32[]{:S(2)}) copy-start(u32[32]{0:T(128)} %constant.73) | copy-start | bytes 388
  78.7 23.4 %copy-start.6 = (s32[8]{0:T(128)S(1)}, s32[8]{0:T(128)}, u32[]{:S(2)}) copy-start(s32[8]{0:T(128)} %param.19) | copy-start | bytes 100
  125.7 18.7 %all-to-all-start = ((bf16[8,8,4096]{2,1,0:T(8,128)(2,1)}), bf16[8,8,4096]{2,1,0:T(8,128)(2,1)S(1)}, u32[]{:S(2)}, u32[]{:S(2)}) async-start(bf16[8,8,4096]{2,1,0:T(8,128)(2,1)} %fusion.12), calls=%async_computation.1 | async-start | bytes 1048576 | tf_op jit(solution)/shard_map/all_to_all | solution.py:41
  144.4 18.6 %all-to-all-start.1 = ((bf16[8,8,4096]{2,1,0:T(8,128)(2,1)}), bf16[8,8,4096]{2,1,0:T(8,128)(2,1)}, u32[]{:S(2)}, u32[]{:S(2)}) async-start(bf16[8,8,4096]{2,1,0:T(8,128)(2,1)} %fusion.13), calls=%async_computation.2 | async-start | bytes 1048576 | tf_op jit(solution)/shard_map/all_to_all | solution.py:42
  148.5 36.3 %all-reduce.3.cloned.1.call-start = ((), (), s32[]{:S(2)}) async-start(), calls=%async_computation.4 | async-start | bytes 262144 | tf_op jit(solution)/shard_map/psum | solution.py:64
  148.6 37.7 %copy-start.3 = (bf16[1024,512]{1,0:T(8,128)(2,1)S(1)}, bf16[1024,512]{1,0:T(8,128)(2,1)}, u32[]{:S(2)}) copy-start(bf16[1024,512]{1,0:T(8,128)(2,1)} %param.12) | copy-start | bytes 3145732
  150.1 36.2 %copy-start.4 = (bf16[1024,512]{1,0:T(8,128)(2,1)S(1)}, bf16[1024,512]{1,0:T(8,128)(2,1)}, u32[]{:S(2)}) copy-start(bf16[1024,512]{1,0:T(8,128)(2,1)} %reduce-scatter.2.cloned.1.call-done) | copy-start | bytes 3145732
Sparse Core Ops, SparseCore 0:
  8.9 37.1 all-gather.2
  99.4 44.3 reduce-scatter.1
  152.7 32.1 all-reduce.2
